TPU v7x, 256 devices: a whole 4x4x8 slice. The times are simulated.
256 devices in a mesh: replica: 16 (over x_hi, z), tensor: 16 (over y, x_lo, core).
Axes of the slice: x: 4 (x_hi: 2, x_lo: 2; x = x_hi * 2 + x_lo), y: 4, z: 8, core: 2. Of those that a mesh axis runs over, the one named last changes fastest.
Arguments:
- hidden: bfloat16 [512, 8192], P('replica'), may hold values from -16 to 16
- q_weight: bfloat16 [8192, 4096], P(None, 'tensor'), may hold values from -0.0625 to 0.0625
- q_gain: float32 [128], replicated, may hold values from 0.1 to 1.9
- o_weight: bfloat16 [4096, 8192], P('tensor'), may hold values from -0.125 to 0.125
- attn_gate: float32 [1], replicated, may hold values from 0.5 to 1.5
- key_codes: bfloat16 [128, 512, 1024], P('replica', 'tensor'), may hold values from -96 to 96
- value_codes: bfloat16 [128, 512, 1024], P('replica', 'tensor'), may hold values from -96 to 96
- key_scales: bfloat16 [128, 16, 8], P('replica', 'tensor'), may hold values from 0.02 to 8
- value_scales: bfloat16 [128, 16, 8], P('replica', 'tensor'), may hold values from 0.019897461 to 0.119628906
- lengths: int32 [128], P('replica'), may hold values from 128 to 512
- dest_replica: int32 [16, 6], replicated, may hold values from 0 to 15, as said below
- move_slot: int32 [16, 6], P('replica'), may hold values from 0 to 7, as said below
Outputs:
- mixed: bfloat16 [512, 8192], P('replica', 'tensor')
- new_keys: bfloat16 [128, 512, 1024], P('replica', 'tensor')
- new_values: bfloat16 [128, 512, 1024], P('replica', 'tensor')
- new_key_scales: bfloat16 [128, 16, 8], P('replica', 'tensor')
- new_value_scales: bfloat16 [128, 16, 8], P('replica', 'tensor')
Inputs may be any that keep to these rules, and one draw needn't show every extreme that they name: For each j the column dest_replica[:, j] names every replica once, so each replica receives exactly 6 requests, at most one from each replica; a request may stay on its own replica. `move_slot`: the 6 slots of one replica are different.
All inputs are finite; a program needn't handle non-finite values.
Results may differ from a plain program's by a relative error of at most 0.0065.
Values may be sent and summed in bfloat16 or wider, within the bound.
No kernel may reach another device: no remote copies, remote signals or barrier semaphores. Data moves between devices by JAX's collectives and lax.ppermute only.
A program may use at most 64 MiB of HBM per device.

v0:
```python
import jax
import jax.numpy as jnp
from jax import lax
from jax.sharding import PartitionSpec as P

NEGATIVE = -1e30
EPSILON = 1e-06


def laid_out(tiles, dim):
    tiles = jnp.moveaxis(tiles, 0, dim)
    shape = tiles.shape
    return tiles.reshape(*shape[:dim], shape[dim] * shape[dim + 1], *shape[dim + 2 :])


def from_everyone(array, axis):
    copies = jnp.broadcast_to(array, (lax.axis_size(axis), *array.shape))
    return lax.all_to_all(copies, axis, split_axis=0, concat_axis=0, tiled=True)


def gather_directly(array, axis, dim):
    return laid_out(from_everyone(array, axis), dim)


def sent_together(arrays, axis, split_dim, concat_dim, along):
    columns = [a.reshape(*a.shape[:along], -1) for a in arrays]
    both = jnp.concatenate(columns, axis=along)
    result, at, done = (
        lax.all_to_all(both, axis, split_axis=split_dim, concat_axis=concat_dim, tiled=True),
        0,
        [],
    )
    for a, column in zip(arrays, columns):
        share = result[..., at : at + column.shape[along]]
        done.append(share.reshape(*share.shape[:along], *a.shape[along:]))
        at += column.shape[along]
    return tuple(done)


def cut_along(array, dim, count):
    before, after = (array.shape[:dim], array.shape[dim + 1 :])
    return jnp.moveaxis(array.reshape(*before, count, -1, *after), dim, 0)


def sent_and_summed(array, axis, dim):
    count = lax.axis_size(axis)
    tiles = lax.all_to_all(cut_along(array, dim, count), axis, 0, 0, tiled=True)
    return jnp.sum(tiles, axis=0)


def outgoing(send_table, codes):
    flat = codes.reshape(codes.shape[0], -1)
    moved = jnp.dot(send_table, flat, preferred_element_type=jnp.float32)
    return moved.astype(jnp.bfloat16).reshape((send_table.shape[0],) + codes.shape[1:])


def incoming(select, keep, received, codes):
    flat = received.reshape(received.shape[0], -1)
    placed = jnp.dot(select, flat, preferred_element_type=jnp.float32).astype(jnp.bfloat16)
    former = codes.reshape(codes.shape[0], -1)
    return jnp.where(keep[:, None], former, placed).reshape(codes.shape)


def attend(
    hidden,
    q_weight,
    q_gain,
    o_weight,
    attn_gate,
    key_codes,
    value_codes,
    key_scales,
    value_scales,
    lengths,
):
    tensors = lax.axis_size("tensor")
    rank = lax.axis_index("tensor")
    held, span, kv_width = key_codes.shape
    kv_heads = key_scales.shape[2]
    head_dim = kv_width // kv_heads
    rows = hidden.shape[0]
    drafts = rows // held
    local_heads = q_weight.shape[1] // head_dim
    projected = jnp.dot(hidden, q_weight, preferred_element_type=jnp.float32).reshape(
        rows, local_heads, head_dim
    )
    projected = projected * lax.rsqrt(
        jnp.mean(projected * projected, axis=-1, keepdims=True) + EPSILON
    )
    query = (projected * q_gain * head_dim ** (-0.5)).astype(jnp.bfloat16)
    every_head = gather_directly(query, "tensor", 1)
    heads = every_head.shape[1]
    grouped = every_head.reshape(held, drafts, kv_heads, heads // kv_heads, head_dim)
    keys = key_codes.reshape(held, span, kv_heads, head_dim)
    values = value_codes.reshape(held, span, kv_heads, head_dim)
    scores = jnp.einsum("rsngd,rtnd->rsngt", grouped, keys, preferred_element_type=jnp.float32)
    scores = scores * key_scales[:, 0, :].astype(jnp.float32)[:, None, :, None, None]
    position = rank * span + jnp.arange(span, dtype=jnp.int32)
    valid = (position[None, :] < lengths[:, None])[:, None, None, None, :]
    block_max = jnp.max(jnp.where(valid, scores, NEGATIVE), axis=-1)
    weights = jnp.where(valid, jnp.exp(scores - block_max[..., None]), 0.0)
    block_sum = jnp.sum(weights, axis=-1)
    block_out = jnp.einsum(
        "rsngt,rtnd->rsngd",
        weights.astype(jnp.bfloat16),
        values,
        preferred_element_type=jnp.float32,
    )
    block_out = block_out * value_scales[:, 0, :].astype(jnp.float32)[:, None, :, None, None]
    partial_value = (
        block_max.reshape(rows, heads),
        block_sum.reshape(rows, heads),
        block_out.reshape(rows, heads, head_dim),
    )
    peaks, totals, pieces = (
        lax.all_to_all(partial_value[0], "tensor", split_axis=1, concat_axis=0, tiled=True),
        *sent_together((partial_value[1], partial_value[2]), "tensor", 1, 0, 2),
    )
    peaks = peaks.reshape(tensors, rows, local_heads)
    top = jnp.max(peaks, axis=0)
    factor = jnp.exp(peaks - top[None])
    total = jnp.sum(totals.reshape(tensors, rows, local_heads) * factor, axis=0)
    summed = jnp.sum(
        pieces.reshape(tensors, rows, local_heads, head_dim) * factor[..., None], axis=0
    )
    attended = (
        (summed / total[..., None]).astype(jnp.bfloat16).reshape(rows, local_heads * head_dim)
    )
    terms = jnp.dot(attended, o_weight, preferred_element_type=jnp.float32)
    shares = sent_and_summed(terms, "tensor", 1)
    width = shares.shape[1]
    residual = lax.dynamic_slice_in_dim(hidden, rank * width, width, 1).astype(jnp.float32)
    return (residual + jnp.tanh(attn_gate[0]) * shares).astype(jnp.bfloat16)


def local(
    hidden,
    q_weight,
    q_gain,
    o_weight,
    attn_gate,
    key_codes,
    value_codes,
    key_scales,
    value_scales,
    lengths,
    dest_replica,
    move_slot,
):
    replicas = lax.axis_size("replica")
    here = lax.axis_index("replica")
    held = key_codes.shape[0]
    slots = move_slot[0]
    own_dest = lax.dynamic_index_in_dim(dest_replica, here, 0, keepdims=False)
    replica_ids = jnp.arange(replicas, dtype=jnp.int32)
    slot_ids = jnp.arange(held, dtype=jnp.int32)
    slot_match = slots[:, None] == slot_ids[None, :]
    send_table = jnp.any(
        (own_dest[:, None, None] == replica_ids[None, :, None]) & slot_match[:, None, :], axis=0
    ).astype(jnp.bfloat16)
    arrive = dest_replica == here
    select = jnp.any(slot_match.T[:, None, :] & arrive[None, :, :], axis=2).astype(jnp.bfloat16)
    keep = jnp.logical_not(jnp.any(slot_match, axis=0))
    received = sent_together(
        (
            outgoing(send_table, key_codes),
            outgoing(send_table, value_codes),
            outgoing(send_table, key_scales),
            outgoing(send_table, value_scales),
        ),
        "replica",
        0,
        0,
        1,
    )
    new_keys = incoming(select, keep, received[0], key_codes)
    new_values = incoming(select, keep, received[1], value_codes)
    new_key_scales = incoming(select, keep, received[2], key_scales)
    new_value_scales = incoming(select, keep, received[3], value_scales)
    mixed = attend(
        hidden,
        q_weight,
        q_gain,
        o_weight,
        attn_gate,
        key_codes,
        value_codes,
        key_scales,
        value_scales,
        lengths,
    )
    return (mixed, new_keys, new_values, new_key_scales, new_value_scales)


def solution(mesh):
    return jax.shard_map(
        local,
        mesh=mesh,
        in_specs=(
            P("replica", None),
            P(None, "tensor"),
            P(),
            P("tensor", None),
            P(),
            P("replica", "tensor", None),
            P("replica", "tensor", None),
            P("replica", "tensor", None),
            P("replica", "tensor", None),
            P("replica"),
            P(),
            P("replica", None),
        ),
        out_specs=(
            P("replica", "tensor"),
            P("replica", "tensor", None),
            P("replica", "tensor", None),
            P("replica", "tensor", None),
            P("replica", "tensor", None),
        ),
        check_vma=False,
    )
```

profile of v0, /device:TPU:32, one launch (start us, length us, event | category | flops | bytes accessed | tf_op | source)
XLA Modules:
  0.0 155.7 jit_solution(13727029361715227020)
XLA Ops:
  0.7 3.2 %fusion.35 = f32[32,256]{1,0:T(8,128)S(1)} fusion(bf16[32,8192]{1,0:T(8,128)(2,1)} %param.12, bf16[8192,256]{1,0:T(8,128)(2,1)} %param.13), kind=kOutput, calls=%fused_computation.72 | convolution fusion | flops 134217728 | bytes 4751360 | tf_op jit(solution)/shard_map/dot_general | solution.py:84
  4.3 0.8 broadcast_in_dim.65
  5.0 5.5 %all-to-all-start = ((bf16[16,32,2,128]{3,1,2,0:T(8,128)(2,1)}), bf16[16,32,2,128]{3,1,2,0:T(8,128)(2,1)S(1)}, u32[]{:S(2)}, u32[]{:S(2)}) async-start(bf16[16,32,2,128]{3,1,2,0:T(8,128)(2,1)} %broadcast_in_dim.65), calls=%async_computation | async-start | bytes 524288 | tf_op jit(solution)/shard_map/all_to_all | solution.py:18
  11.0 7.6 %all-to-all-done = bf16[16,32,2,128]{3,1,2,0:T(8,128)(2,1)S(1)} async-done(((bf16[16,32,2,128]{3,1,2,0:T(8,128)(2,1)}), bf16[16,32,2,128]{3,1,2,0:T(8,128)(2,1)S(1)}, u32[]{:S(2)}, u32[]{:S(2)}) %all-to-all-start) | async-done | bytes 262176 | tf_op jit(solution)/shard_map/all_to_all | solution.py:18
  18.5 0.6 select_reduce_fusion
  19.1 0.8 fusion.15
  19.9 0.6 fusion.4
  21.1 1.6 %copy.145 = f32[32,32,129]{2,0,1:T(8,128)} copy(f32[32,32,129]{2,1,0:T(8,128)S(1)} %pad_maximum_fusion) | data formatting | bytes 1056768 | tf_op jit(solution)/shard_map/concatenate | solution.py:27
  22.7 3.7 %all-to-all-start.1 = ((f32[32,32,129]{2,0,1:T(8,128)}), f32[32,32,129]{2,0,1:T(8,128)S(1)}, u32[]{:S(2)}, u32[]{:S(2)}) async-start(f32[32,32,129]{2,0,1:T(8,128)} %copy.145), calls=%async_computation.1 | async-start | bytes 2097152 | tf_op jit(solution)/shard_map/all_to_all | solution.py:29
  26.4 6.4 %copy.163 = bf16[8192,256]{1,0:T(8,128)(2,1)} copy(bf16[8192,256]{0,1:T(8,128)(2,1)} %bitcast.112) | data formatting | bytes 8388608 | tf_op jit(solution)/shard_map/dot_general | solution.py:129
  33.1 0.5 copy.147
  33.6 0.7 all_to_all.44
  34.4 8.5 %all-to-all-done.1 = f32[32,32,129]{2,0,1:T(8,128)S(1)} async-done(((f32[32,32,129]{2,0,1:T(8,128)}), f32[32,32,129]{2,0,1:T(8,128)S(1)}, u32[]{:S(2)}, u32[]{:S(2)}) %all-to-all-start.1) | async-done | bytes 528416 | tf_op jit(solution)/shard_map/all_to_all | solution.py:29
  42.9 3.5 %all-to-all-start.2 = ((f32[32,16,2]{0,2,1:T(2,128)}), f32[32,16,2]{0,2,1:T(2,128)S(1)}, u32[]{:S(2)}, u32[]{:S(2)}) async-start(f32[32,16,2]{0,2,1:T(2,128)} %all_to_all.44), calls=%async_computation.2 | async-start | bytes 32768 | tf_op jit(solution)/shard_map/all_to_all | solution.py:116
  46.9 5.4 %all-to-all-done.2 = f32[32,16,2]{0,2,1:T(2,128)S(1)} async-done(((f32[32,16,2]{0,2,1:T(2,128)}), f32[32,16,2]{0,2,1:T(2,128)S(1)}, u32[]{:S(2)}, u32[]{:S(2)}) %all-to-all-start.2) | async-done | bytes 4128 | tf_op jit(solution)/shard_map/all_to_all | solution.py:116
  52.8 4.5 %convolution_bitcast_fusion = f32[16,32,512]{2,1,0:T(8,128)} fusion(bf16[32,256,1]{1,0,2:T(8,128)(2,1)S(1)} %reshape.208, bf16[16,512,256]{2,1,0:T(8,128)(2,1)} %bitcast.102), kind=kOutput, calls=%fused_computation.9 | convolution fusion | flops 134217728 | bytes 5259264 | tf_op jit(solution)/shard_map/dot_general | solution.py:129
  57.3 4.4 %all-to-all-start.3 = ((f32[16,32,512]{2,1,0:T(8,128)}), f32[16,32,512]{2,1,0:T(8,128)}, u32[]{:S(2)}, u32[]{:S(2)}) async-start(f32[16,32,512]{2,1,0:T(8,128)} %convolution_bitcast_fusion), calls=%async_computation.3 | async-start | bytes 2097152 | tf_op jit(solution)/shard_map/all_to_all | solution.py:47
  64.3 1.4 copy-done
  65.6 0.5 broadcast.80
  66.1 3.9 %reduce.4 = bf16[16,65552]{1,0:T(8,128)(2,1)S(1)} reduce(bf16[16,1,65552]{2,0,1:T(8,128)(2,1)} %bitcast.107, bf16[]{:T(256)} %broadcast.80), dimensions={1}, to_apply=%copy.154.reduce_sub_computation | reduce | bytes 4195330 | tf_op jit(solution)/shard_map/all_to_all | solution.py:29
  70.0 2.5 %reshape.212 = bf16[16,2,32776]{2,1,0:T(2,128)(2,1)} reshape(bf16[16,65552]{1,0:T(8,128)(2,1)S(1)} %reduce.4) | data formatting | bytes 4195328
  72.5 5.7 %all-to-all-done.3 = f32[16,32,512]{2,1,0:T(8,128)} async-done(((f32[16,32,512]{2,1,0:T(8,128)}), f32[16,32,512]{2,1,0:T(8,128)}, u32[]{:S(2)}, u32[]{:S(2)}) %all-to-all-start.3) | async-done | bytes 1048608 | tf_op jit(solution)/shard_map/all_to_all | solution.py:47
  78.2 10.7 %all-to-all-start.4 = ((bf16[16,2,32776]{2,1,0:T(2,128)(2,1)}), bf16[16,2,32776]{2,1,0:T(2,128)(2,1)S(1)}, u32[]{:S(2)}, u32[]{:S(2)}) async-start(bf16[16,2,32776]{2,1,0:T(2,128)(2,1)} %reshape.212), calls=%async_computation.4 | async-start | bytes 4210688 | tf_op jit(solution)/shard_map/all_to_all | solution.py:29
  89.8 1.3 reduce_sum.49
  91.1 1.4 add_convert_fusion
  92.5 46.7 %all-to-all-done.4 = bf16[16,2,32776]{2,1,0:T(2,128)(2,1)S(1)} async-done(((bf16[16,2,32776]{2,1,0:T(2,128)(2,1)}), bf16[16,2,32776]{2,1,0:T(2,128)(2,1)S(1)}, u32[]{:S(2)}, u32[]{:S(2)}) %all-to-all-start.4) | async-done | bytes 2097696 | tf_op jit(solution)/shard_map/all_to_all | solution.py:29
  139.2 9.9 %reshape.213 = bf16[16,1,65552]{2,1,0:T(2,128)(2,1)} reshape(bf16[16,2,32776]{2,1,0:T(2,128)(2,1)S(1)} %all-to-all-done.4) | data formatting | bytes 4195328
  149.1 2.4 %copy.190 = bf16[16,1,65552]{2,0,1:T(8,128)(2,1)S(1)} copy(bf16[16,1,65552]{2,1,0:T(2,128)(2,1)} %reshape.213) | data formatting | bytes 4195328
  152.1 0.8 fusion.9
  152.9 0.7 fusion.7
  153.6 1.1 copy.156
  154.7 1.1 copy.155
  (63 shorter events, 5.9 us)
Async XLA Ops:
  0.6 3.5 %copy-start.6 = (f32[128]{0:T(128)S(1)}, f32[128]{0:T(128)}, u32[]{:S(2)}) copy-start(f32[128]{0:T(128)} %param.14) | copy-start | bytes 1540
  0.6 9.9 %copy-start.5 = (bf16[8,1,8]{2,0,1:T(8,128)(2,1)S(1)}, bf16[8,1,8]{2,0,1:T(8,128)(2,1)}, u32[]{:S(2)}) copy-start(bf16[8,1,8]{2,0,1:T(8,128)(2,1)} %param.19) | copy-start | bytes 388
  0.7 9.9 %copy-start.4 = (bf16[8,1,8]{2,0,1:T(8,128)(2,1)S(1)}, bf16[8,1,8]{2,0,1:T(8,128)(2,1)}, u32[]{:S(2)}) copy-start(bf16[8,1,8]{2,0,1:T(8,128)(2,1)} %param.20) | copy-start | bytes 388
  0.7 9.9 %copy-start.1 = (bf16[8,32,1024]{2,1,0:T(8,128)(2,1)S(1)}, bf16[8,32,1024]{2,1,0:T(8,128)(2,1)}, u32[]{:S(2)}) copy-start(bf16[8,32,1024]{2,1,0:T(8,128)(2,1)} %param.18) | copy-start | bytes 1572868
  3.9 6.8 %copy-start.2 = (bf16[8,32,1024]{2,1,0:T(8,128)(2,1)S(1)}, bf16[8,32,1024]{2,1,0:T(8,128)(2,1)}, u32[]{:S(2)}) copy-start(bf16[8,32,1024]{2,1,0:T(8,128)(2,1)} %param.17) | copy-start | bytes 1572868
  3.9 6.9 %copy-start.7 = (s32[8]{0:T(128)S(1)}, s32[8]{0:T(128)}, u32[]{:S(2)}) copy-start(s32[8]{0:T(128)} %param.21) | copy-start | bytes 100
  5.0 13.5 %all-to-all-start = ((bf16[16,32,2,128]{3,1,2,0:T(8,128)(2,1)}), bf16[16,32,2,128]{3,1,2,0:T(8,128)(2,1)S(1)}, u32[]{:S(2)}, u32[]{:S(2)}) async-start(bf16[16,32,2,128]{3,1,2,0:T(8,128)(2,1)} %broadcast_in_dim.65), calls=%async_computation | async-start | bytes 524288 | tf_op jit(solution)/shard_map/all_to_all | solution.py:18
  22.7 20.2 %all-to-all-start.1 = ((f32[32,32,129]{2,0,1:T(8,128)}), f32[32,32,129]{2,0,1:T(8,128)S(1)}, u32[]{:S(2)}, u32[]{:S(2)}) async-start(f32[32,32,129]{2,0,1:T(8,128)} %copy.145), calls=%async_computation.1 | async-start | bytes 2097152 | tf_op jit(solution)/shard_map/all_to_all | solution.py:29
  26.4 6.4 %copy-start.3 = (s32[16,6]{0,1:T(8,128)S(1)}, s32[16,6]{0,1:T(8,128)}, u32[]{:S(2)}) copy-start(s32[16,6]{0,1:T(8,128)} %param.22) | copy-start | bytes 1156
  26.4 6.7 %copy-start.8 = (s32[1,6]{1,0:T(1,128)S(1)}, s32[1,6]{1,0:T(1,128)}, u32[]{:S(2)}) copy-start(s32[1,6]{1,0:T(1,128)} %param.23) | copy-start | bytes 76
  42.9 9.5 %all-to-all-start.2 = ((f32[32,16,2]{0,2,1:T(2,128)}), f32[32,16,2]{0,2,1:T(2,128)S(1)}, u32[]{:S(2)}, u32[]{:S(2)}) async-start(f32[32,16,2]{0,2,1:T(2,128)} %all_to_all.44), calls=%async_computation.2 | async-start | bytes 32768 | tf_op jit(solution)/shard_map/all_to_all | solution.py:116
  57.3 20.9 %all-to-all-start.3 = ((f32[16,32,512]{2,1,0:T(8,128)}), f32[16,32,512]{2,1,0:T(8,128)}, u32[]{:S(2)}, u32[]{:S(2)}) async-start(f32[16,32,512]{2,1,0:T(8,128)} %convolution_bitcast_fusion), calls=%async_computation.3 | async-start | bytes 2097152 | tf_op jit(solution)/shard_map/all_to_all | solution.py:47
  64.3 1.4 copy-start
  78.2 61.0 %all-to-all-start.4 = ((bf16[16,2,32776]{2,1,0:T(2,128)(2,1)}), bf16[16,2,32776]{2,1,0:T(2,128)(2,1)S(1)}, u32[]{:S(2)}, u32[]{:S(2)}) async-start(bf16[16,2,32776]{2,1,0:T(2,128)(2,1)} %reshape.212), calls=%async_computation.4 | async-start | bytes 4210688 | tf_op jit(solution)/shard_map/all_to_all | solution.py:29
where the time goes:
time: 157 us; the launch traced here: 156 us
  waiting for transfers between devices  73.9 us (47%)
  local copies, waits for them, and re-layouts  31.4 us (20%)
  starting transfers between devices  27.7 us (18%)
  matrix products  12.2 us (8%)
  other arithmetic  8.71 us (6%)
  between operations  1.72 us (1%)
    all_to_all x2, waiting for transfers between devices, sent_together(): lax.all_to_all(both, axis, split_axis=split_dim, concat_axis=concat_dim,...  55.2 us
    unnamed x28, local copies, waits for them, and re-layouts  19.3 us
    all_to_all x2, starting transfers between devices, sent_together(): lax.all_to_all(both, axis, split_axis=split_dim, concat_axis=concat_dim,...  14.4 us
    all_to_all x1, waiting for transfers between devices, from_everyone(): return lax.all_to_all(copies, axis, split_axis=0, concat_axis=0, tiled=True)  7.57 us
    dot_general x1, local copies, waits for them, and re-layouts, attend(): terms = jnp.dot(attended, o_weight, preferred_element_type=jnp.float32)  6.4 us
    all_to_all x1, waiting for transfers between devices, sent_and_summed(): tiles = lax.all_to_all(cut_along(array, dim, count), axis, 0, 0, tiled=True)  5.73 us
    all_to_all x1, starting transfers between devices, from_everyone(): return lax.all_to_all(copies, axis, split_axis=0, concat_axis=0, tiled=True)  5.5 us
    all_to_all x1, waiting for transfers between devices, attend(): lax.all_to_all(partial_value[0], 'tensor', split_axis=1, concat_axis=0, t...  5.44 us
  transfers between devices with their start and end apart: 5, of which 5 were waited for; matrix products, arithmetic and copies ran while one was open for 13% of the time, Pallas kernels for 0%

commit v1 on v0

--- a/solution.py
+++ b/solution.py
@@ -112,8 +112,17 @@
         block_sum.reshape(rows, heads),
         block_out.reshape(rows, heads, head_dim),
     )
+
+    def core_direct(x_local):
+        return jnp.concatenate(
+            lax.all_to_all(
+                jnp.stack(jnp.split(x_local, lax.psum(1, "tensor"), axis=1)), "tensor", 0, 0
+            ),
+            axis=0,
+        )
+
     peaks, totals, pieces = (
-        lax.all_to_all(partial_value[0], "tensor", split_axis=1, concat_axis=0, tiled=True),
+        core_direct(partial_value[0]),
         *sent_together((partial_value[1], partial_value[2]), "tensor", 1, 0, 2),
     )
     peaks = peaks.reshape(tensors, rows, local_heads)

time: 157 us -> 166 us (1.057)
  local copies, waits for them, and re-layouts: 31.4 us -> 40.7 us
    unnamed x28 -> x43, local copies, waits for them, and re-layouts: 19.3 us -> 27.8 us
where the time goes in v1:
time: 166 us; the launch traced here: 165 us
  waiting for transfers between devices  73.6 us (44%)
  local copies, waits for them, and re-layouts  40.7 us (25%)
  starting transfers between devices  27.8 us (17%)
  matrix products  12.2 us (7%)
  other arithmetic  8.7 us (5%)
  between operations  1.75 us (1%)
    all_to_all x2, waiting for transfers between devices, sent_together(): lax.all_to_all(both, axis, split_axis=split_dim, concat_axis=concat_dim,...  56.4 us
    unnamed x43, local copies, waits for them, and re-layouts  27.8 us
    all_to_all x2, starting transfers between devices, sent_together(): lax.all_to_all(both, axis, split_axis=split_dim, concat_axis=concat_dim,...  14.4 us
    all_to_all x1, waiting for transfers between devices, from_everyone(): return lax.all_to_all(copies, axis, split_axis=0, concat_axis=0, tiled=True)  7.57 us
    dot_general x1, local copies, waits for them, and re-layouts, attend(): terms = jnp.dot(attended, o_weight, preferred_element_type=jnp.float32)  6.4 us
    all_to_all x1, waiting for transfers between devices, sent_and_summed(): tiles = lax.all_to_all(cut_along(array, dim, count), axis, 0, 0, tiled=True)  5.73 us
    all_to_all x1, starting transfers between devices, from_everyone(): return lax.all_to_all(copies, axis, split_axis=0, concat_axis=0, tiled=True)  5.5 us
    dot_general x1, matrix products, attend(): terms = jnp.dot(attended, o_weight, preferred_element_type=jnp.float32)  4.49 us
  transfers between devices with their start and end apart: 5, of which 5 were waited for; matrix products, arithmetic and copies ran while one was open for 13% of the time, Pallas kernels for 0%

profile of v1, /device:TPU:32, one launch (start us, length us, event | category | flops | bytes accessed | tf_op | source)
XLA Modules:
  0.0 164.8 jit_solution(12785828334617476455)
XLA Ops:
  0.7 3.2 %fusion.33 = f32[32,256]{1,0:T(8,128)S(1)} fusion(bf16[32,8192]{1,0:T(8,128)(2,1)} %param.12, bf16[8192,256]{1,0:T(8,128)(2,1)} %param.13), kind=kOutput, calls=%fused_computation.84 | convolution fusion | flops 134217728 | bytes 4751360 | tf_op jit(solution)/shard_map/dot_general | solution.py:84
  4.3 0.8 broadcast_in_dim.65
  5.0 5.5 %all-to-all-start = ((bf16[16,32,2,128]{3,1,2,0:T(8,128)(2,1)}), bf16[16,32,2,128]{3,1,2,0:T(8,128)(2,1)S(1)}, u32[]{:S(2)}, u32[]{:S(2)}) async-start(bf16[16,32,2,128]{3,1,2,0:T(8,128)(2,1)} %broadcast_in_dim.65), calls=%async_computation | async-start | bytes 524288 | tf_op jit(solution)/shard_map/all_to_all | solution.py:18
  11.0 7.6 %all-to-all-done = bf16[16,32,2,128]{3,1,2,0:T(8,128)(2,1)S(1)} async-done(((bf16[16,32,2,128]{3,1,2,0:T(8,128)(2,1)}), bf16[16,32,2,128]{3,1,2,0:T(8,128)(2,1)S(1)}, u32[]{:S(2)}, u32[]{:S(2)}) %all-to-all-start) | async-done | bytes 262176 | tf_op jit(solution)/shard_map/all_to_all | solution.py:18
  19.1 0.8 fusion.15
  20.0 0.6 fusion.4
  22.1 0.6 constant_dynamic-update-slice_fusion.15
  25.0 0.6 constant_dynamic-update-slice_fusion.10
  25.5 0.6 constant_dynamic-update-slice_fusion.9
  26.1 0.6 constant_dynamic-update-slice_fusion.8
  31.2 3.5 %all-to-all-start.2 = ((f32[16,32,2]{1,2,0:T(2,128)}), f32[16,32,2]{1,2,0:T(2,128)S(1)}, u32[]{:S(2)}, u32[]{:S(2)}) async-start(f32[16,32,2]{1,2,0:T(2,128)} %constant_dynamic-update-slice_fusion), calls=%async_computation.2 | async-start | bytes 32768 | tf_op jit(solution)/shard_map/all_to_all | solution.py:118
  35.2 1.6 copy.273
  36.8 3.9 %all-to-all-done.2 = f32[16,32,2]{1,2,0:T(2,128)S(1)} async-done(((f32[16,32,2]{1,2,0:T(2,128)}), f32[16,32,2]{1,2,0:T(2,128)S(1)}, u32[]{:S(2)}, u32[]{:S(2)}) %all-to-all-start.2) | async-done | bytes 4128 | tf_op jit(solution)/shard_map/all_to_all | solution.py:118
  40.7 3.7 %all-to-all-start.1 = ((f32[32,32,129]{2,0,1:T(8,128)}), f32[32,32,129]{2,0,1:T(8,128)S(1)}, u32[]{:S(2)}, u32[]{:S(2)}) async-start(f32[32,32,129]{2,0,1:T(8,128)} %copy.273), calls=%async_computation.1 | async-start | bytes 2097152 | tf_op jit(solution)/shard_map/all_to_all | solution.py:29
  44.4 6.4 %copy.307 = bf16[8192,256]{1,0:T(8,128)(2,1)} copy(bf16[8192,256]{0,1:T(8,128)(2,1)} %bitcast.132) | data formatting | bytes 8388608 | tf_op jit(solution)/shard_map/dot_general | solution.py:138
  51.2 9.7 %all-to-all-done.1 = f32[32,32,129]{2,0,1:T(8,128)S(1)} async-done(((f32[32,32,129]{2,0,1:T(8,128)}), f32[32,32,129]{2,0,1:T(8,128)S(1)}, u32[]{:S(2)}, u32[]{:S(2)}) %all-to-all-start.1) | async-done | bytes 528416 | tf_op jit(solution)/shard_map/all_to_all | solution.py:29
  61.8 4.5 %convolution_bitcast_fusion = f32[16,32,512]{2,1,0:T(8,128)} fusion(bf16[32,256,1]{1,0,2:T(8,128)(2,1)S(1)} %reshape.205, bf16[16,512,256]{2,1,0:T(8,128)(2,1)} %bitcast.122), kind=kOutput, calls=%fused_computation.9 | convolution fusion | flops 134217728 | bytes 5259264 | tf_op jit(solution)/shard_map/dot_general | solution.py:138
  66.3 4.4 %all-to-all-start.3 = ((f32[16,32,512]{2,1,0:T(8,128)}), f32[16,32,512]{2,1,0:T(8,128)}, u32[]{:S(2)}, u32[]{:S(2)}) async-start(f32[16,32,512]{2,1,0:T(8,128)} %convolution_bitcast_fusion), calls=%async_computation.3 | async-start | bytes 2097152 | tf_op jit(solution)/shard_map/all_to_all | solution.py:47
  73.3 1.4 copy-done
  75.1 3.9 %reduce.4 = bf16[16,65552]{1,0:T(8,128)(2,1)S(1)} reduce(bf16[16,1,65552]{2,0,1:T(8,128)(2,1)} %bitcast.127, bf16[]{:T(256)} %broadcast.80), dimensions={1}, to_apply=%copy.298.reduce_sub_computation | reduce | bytes 4195330 | tf_op jit(solution)/shard_map/all_to_all | solution.py:29
  79.0 2.5 %reshape.209 = bf16[16,2,32776]{2,1,0:T(2,128)(2,1)} reshape(bf16[16,65552]{1,0:T(8,128)(2,1)S(1)} %reduce.4) | data formatting | bytes 4195328
  81.5 5.7 %all-to-all-done.3 = f32[16,32,512]{2,1,0:T(8,128)} async-done(((f32[16,32,512]{2,1,0:T(8,128)}), f32[16,32,512]{2,1,0:T(8,128)}, u32[]{:S(2)}, u32[]{:S(2)}) %all-to-all-start.3) | async-done | bytes 1048608 | tf_op jit(solution)/shard_map/all_to_all | solution.py:47
  87.2 10.8 %all-to-all-start.4 = ((bf16[16,2,32776]{2,1,0:T(2,128)(2,1)}), bf16[16,2,32776]{2,1,0:T(2,128)(2,1)S(1)}, u32[]{:S(2)}, u32[]{:S(2)}) async-start(bf16[16,2,32776]{2,1,0:T(2,128)(2,1)} %reshape.209), calls=%async_computation.4 | async-start | bytes 4210688 | tf_op jit(solution)/shard_map/all_to_all | solution.py:29
  98.8 1.3 reduce_sum.49
  100.1 1.4 add_convert_fusion
  101.5 46.7 %all-to-all-done.4 = bf16[16,2,32776]{2,1,0:T(2,128)(2,1)S(1)} async-done(((bf16[16,2,32776]{2,1,0:T(2,128)(2,1)}), bf16[16,2,32776]{2,1,0:T(2,128)(2,1)S(1)}, u32[]{:S(2)}, u32[]{:S(2)}) %all-to-all-start.4) | async-done | bytes 2097696 | tf_op jit(solution)/shard_map/all_to_all | solution.py:29
  148.2 9.9 %reshape.210 = bf16[16,1,65552]{2,1,0:T(2,128)(2,1)} reshape(bf16[16,2,32776]{2,1,0:T(2,128)(2,1)S(1)} %all-to-all-done.4) | data formatting | bytes 4195328
  158.1 2.4 %copy.331 = bf16[16,1,65552]{2,0,1:T(8,128)(2,1)S(1)} copy(bf16[16,1,65552]{2,1,0:T(2,128)(2,1)} %reshape.210) | data formatting | bytes 4195328
  161.1 0.8 fusion.9
  161.9 0.7 fusion.7
  162.6 1.1 copy.300
  163.7 1.1 copy.299
  (97 shorter events, 15.2 us)
Async XLA Ops:
  0.6 3.5 %copy-start.6 = (f32[128]{0:T(128)S(1)}, f32[128]{0:T(128)}, u32[]{:S(2)}) copy-start(f32[128]{0:T(128)} %param.14) | copy-start | bytes 1540
  0.6 9.9 %copy-start.5 = (bf16[8,1,8]{2,0,1:T(8,128)(2,1)S(1)}, bf16[8,1,8]{2,0,1:T(8,128)(2,1)}, u32[]{:S(2)}) copy-start(bf16[8,1,8]{2,0,1:T(8,128)(2,1)} %param.19) | copy-start | bytes 388
  0.7 9.9 %copy-start.4 = (bf16[8,1,8]{2,0,1:T(8,128)(2,1)S(1)}, bf16[8,1,8]{2,0,1:T(8,128)(2,1)}, u32[]{:S(2)}) copy-start(bf16[8,1,8]{2,0,1:T(8,128)(2,1)} %param.20) | copy-start | bytes 388
  0.7 9.9 %copy-start.1 = (bf16[8,32,1024]{2,1,0:T(8,128)(2,1)S(1)}, bf16[8,32,1024]{2,1,0:T(8,128)(2,1)}, u32[]{:S(2)}) copy-start(bf16[8,32,1024]{2,1,0:T(8,128)(2,1)} %param.18) | copy-start | bytes 1572868
  3.9 6.8 %copy-start.2 = (bf16[8,32,1024]{2,1,0:T(8,128)(2,1)S(1)}, bf16[8,32,1024]{2,1,0:T(8,128)(2,1)}, u32[]{:S(2)}) copy-start(bf16[8,32,1024]{2,1,0:T(8,128)(2,1)} %param.17) | copy-start | bytes 1572868
  3.9 6.9 %copy-start.7 = (s32[8]{0:T(128)S(1)}, s32[8]{0:T(128)}, u32[]{:S(2)}) copy-start(s32[8]{0:T(128)} %param.21) | copy-start | bytes 100
  5.0 13.5 %all-to-all-start = ((bf16[16,32,2,128]{3,1,2,0:T(8,128)(2,1)}), bf16[16,32,2,128]{3,1,2,0:T(8,128)(2,1)S(1)}, u32[]{:S(2)}, u32[]{:S(2)}) async-start(bf16[16,32,2,128]{3,1,2,0:T(8,128)(2,1)} %broadcast_in_dim.65), calls=%async_computation | async-start | bytes 524288 | tf_op jit(solution)/shard_map/all_to_all | solution.py:18
  31.2 9.5 %all-to-all-start.2 = ((f32[16,32,2]{1,2,0:T(2,128)}), f32[16,32,2]{1,2,0:T(2,128)S(1)}, u32[]{:S(2)}, u32[]{:S(2)}) async-start(f32[16,32,2]{1,2,0:T(2,128)} %constant_dynamic-update-slice_fusion), calls=%async_computation.2 | async-start | bytes 32768 | tf_op jit(solution)/shard_map/all_to_all | solution.py:118
  40.7 20.2 %all-to-all-start.1 = ((f32[32,32,129]{2,0,1:T(8,128)}), f32[32,32,129]{2,0,1:T(8,128)S(1)}, u32[]{:S(2)}, u32[]{:S(2)}) async-start(f32[32,32,129]{2,0,1:T(8,128)} %copy.273), calls=%async_computation.1 | async-start | bytes 2097152 | tf_op jit(solution)/shard_map/all_to_all | solution.py:29
  44.3 6.4 %copy-start.3 = (s32[16,6]{0,1:T(8,128)S(1)}, s32[16,6]{0,1:T(8,128)}, u32[]{:S(2)}) copy-start(s32[16,6]{0,1:T(8,128)} %param.22) | copy-start | bytes 1156
  44.4 6.7 %copy-start.8 = (s32[1,6]{1,0:T(1,128)S(1)}, s32[1,6]{1,0:T(1,128)}, u32[]{:S(2)}) copy-start(s32[1,6]{1,0:T(1,128)} %param.23) | copy-start | bytes 76
  66.3 20.9 %all-to-all-start.3 = ((f32[16,32,512]{2,1,0:T(8,128)}), f32[16,32,512]{2,1,0:T(8,128)}, u32[]{:S(2)}, u32[]{:S(2)}) async-start(f32[16,32,512]{2,1,0:T(8,128)} %convolution_bitcast_fusion), calls=%async_computation.3 | async-start | bytes 2097152 | tf_op jit(solution)/shard_map/all_to_all | solution.py:47
  73.3 1.4 copy-start
  87.2 61.0 %all-to-all-start.4 = ((bf16[16,2,32776]{2,1,0:T(2,128)(2,1)}), bf16[16,2,32776]{2,1,0:T(2,128)(2,1)S(1)}, u32[]{:S(2)}, u32[]{:S(2)}) async-start(bf16[16,2,32776]{2,1,0:T(2,128)(2,1)} %reshape.209), calls=%async_computation.4 | async-start | bytes 4210688 | tf_op jit(solution)/shard_map/all_to_all | solution.py:29
